TPU v7x, 256 devices: a whole 4x4x8 slice. The times are simulated.
256 devices in a mesh: gx: 8 (over x, z_lo), gy: 8 (over z_hi, core), gz: 4 (over y).
Axes of the slice: x: 4, y: 4, z: 8 (z_hi: 4, z_lo: 2; z = z_hi * 2 + z_lo), core: 2. Of those that a mesh axis runs over, the one named last changes fastest.
Arguments:
- partials: float32 [32, 128, 128, 512], P('gx', None, 'gy', 'gz'), may hold values from -40 to 40
- code_bits: int32 [32, 128], replicated, may hold values from 0 to 1
- group_map: int32 [32], replicated, may hold values from 0 to 31, each once
- velocity: float32 [128, 128, 512], P('gx', 'gy', 'gz'), may hold values from 1.5 to 4.5
Outputs:
- gradient: float32 [128, 128, 512], P('gx', 'gy', 'gz')
- new_model: float32 [128, 128, 512], P('gx', 'gy', 'gz')
Inputs may be any that keep to these rules, and one draw needn't show every extreme that they name: `group_map`: every group of 0 to 31 stands in exactly one slot.
All inputs are finite; a program needn't handle non-finite values.
Results may differ from a plain program's by a relative error of at most 0.0001.
Values sent between devices are 32-bit elements; how exact they have to be, the bound alone decides.
A program may use at most 64 MiB of HBM per device.

v0:
```python
import functools

import jax
import jax.numpy as jnp
from jax import lax
from jax.experimental import pallas as pl
from jax.experimental.pallas import tpu as pltpu
from jax.sharding import PartitionSpec as P

ITERS = 3
H = ITERS
SEG = 16
PIECES = 4

step_length = 0.5
tv_weight = 0.2
dual_step = 0.28
primal_step = 0.28
MESH = pl.DeviceIdType.MESH


def geometry(dims):
    nx, ny, nz, slots, bx, by, bz = dims
    win = bx + H * min(2, nx - 1)
    tiles = -(-win // (bz // SEG))
    yp = -(-(by + 2 * H) // 8) * 8
    return win, tiles, yp, 16 + (win + tiles) * yp


def own_offset(nx, bx, win, q):
    if nx == 1:
        return 0
    return jnp.where(q == 0, 0, jnp.where(q == nx - 1, win - bx, H))


def roll(value, shift):
    shift = shift % value.shape[1]
    return value if shift == 0 else pltpu.roll(value, shift, 1)


def kernel(
    dims,
    partials,
    code_bits,
    group_map,
    velocity,
    va,
    ga,
    gw,
    scale_out,
    bits,
    gmap,
    part,
    psum,
    vw,
    xr,
    xh,
    ys,
    yr,
    ss,
    zr,
    ds,
    dr,
    za,
    ar,
    in_sem,
    part_sem,
    xs_sem,
    xr_sem,
    xhs_sem,
    xhr_sem,
    vs_sem,
    vr_sem,
    hs_sem,
    hr_sem,
    ars_sem,
    arr_sem,
    chain_sem,
):
    nx, ny, nz, slots, bx, by, bz = dims
    win, tiles, yp, flat = geometry(dims)
    groups = bz // SEG
    ix, iy, iz = lax.axis_index("gx"), lax.axis_index("gy"), lax.axis_index("gz")
    offset = functools.partial(own_offset, nx, bx, win)
    off = offset(ix)
    size = bx // PIECES
    order = [(d, p) for d in list(range(1, nx)) + [0] for p in range(PIECES)]

    def first_row(d, p):
        return lax.rem(ix + d, nx) * bx + p * size

    in_copies = [
        pltpu.make_async_copy(code_bits, bits, in_sem.at[0]),
        pltpu.make_async_copy(group_map, gmap, in_sem.at[1]),
    ]
    v_copy = pltpu.make_async_copy(velocity, vw.at[pl.ds(off, bx)], in_sem.at[2])
    for c in in_copies:
        c.start()
    v_copy.start()
    part_copies = []
    for n, (d, p) in enumerate(order):
        where = pl.ds(first_row(d, p), size)
        part_copies.append(
            pltpu.make_async_copy(partials.at[:, where], part.at[:, where], part_sem.at[n])
        )
    for c in part_copies:
        c.start()

    barrier = pltpu.get_barrier_semaphore()

    def at(x=None, y=None, z=None):
        return (ix if x is None else x, iy if y is None else y, iz if z is None else z)

    def notify(sem, device):
        pl.semaphore_signal(sem, inc=1, device_id=device, device_id_type=MESH)

    for buffer in (yr, zr, dr):
        buffer[...] = jnp.zeros_like(buffer)

    for d in range(1, nx):
        notify(barrier, at(x=lax.rem(ix + d, nx)))
    has = {
        "y-": iy > 0,
        "y+": iy < ny - 1,
        "z-": iz > 0,
        "z+": iz < nz - 1,
    }
    near = {
        "y-": at(y=iy - 1),
        "y+": at(y=iy + 1),
        "z-": at(z=iz - 1),
        "z+": at(z=iz + 1),
    }
    total = jnp.int32(nx - 1)
    for key in has:
        total = total + has[key].astype(jnp.int32)

        @pl.when(has[key])
        def _(key=key):
            notify(barrier, near[key])

    for buffer in (za, va, ga):
        buffer[...] = jnp.zeros_like(buffer)
    pl.semaphore_wait(barrier, total)

    def v_halo(side):
        q = ix + 1 if side == 0 else ix - 1
        src = off + bx - H if side == 0 else off
        dst = offset(q) - H if side == 0 else offset(q) + bx
        return pltpu.make_async_remote_copy(
            src_ref=vw.at[pl.ds(src, H)],
            dst_ref=vw.at[pl.ds(dst, H)],
            send_sem=vs_sem.at[side],
            recv_sem=vr_sem.at[side],
            device_id=at(x=q),
            device_id_type=MESH,
        )

    v_copy.wait()
    if nx > 1:
        @pl.when(ix < nx - 1)
        def _():
            v_halo(0).start()

        @pl.when(ix > 0)
        def _():
            v_halo(1).start()

    for c in in_copies:
        c.wait()
    codes = [gmap[ix * slots + s] for s in range(slots)]

    def reduce_rows(first):
        def one(r, carry):
            row = first + r
            acc = None
            for s in range(slots):
                sign = (2 * bits[codes[s], row] - 1).astype(jnp.float32)
                term = sign * part[s, row]
                acc = term if acc is None else acc + term
            psum[row] = acc
            return carry

        lax.fori_loop(0, size, one, 0, unroll=2)

    def x_copy(d, p):
        return pltpu.make_async_remote_copy(
            src_ref=psum.at[pl.ds(first_row(d, p), size)],
            dst_ref=xr.at[d - 1, pl.ds(p * size, size)],
            send_sem=xs_sem.at[d - 1, p],
            recv_sem=xr_sem.at[d - 1, p],
            device_id=at(x=lax.rem(ix + d, nx)),
            device_id_type=MESH,
        )

    for n, (d, p) in enumerate(order):
        part_copies[n].wait()
        reduce_rows(first_row(d, p))
        if d > 0:
            x_copy(d, p).start()

    def halo_copy(d, side):
        q = lax.rem(ix + d, nx)
        first = q * bx - H if side == 0 else q * bx + bx
        return pltpu.make_async_remote_copy(
            src_ref=psum.at[pl.ds(first, H)],
            dst_ref=xh.at[d - 1, side],
            send_sem=xhs_sem.at[d - 1, side],
            recv_sem=xhr_sem.at[d - 1, side],
            device_id=at(x=q),
            device_id_type=MESH,
        )

    for d in range(1, nx):
        q = lax.rem(ix + d, nx)

        @pl.when(q > 0)
        def _(d=d):
            halo_copy(d, 0).start()

        @pl.when(q < nx - 1)
        def _(d=d):
            halo_copy(d, 1).start()

    def chain(up, down, count, index, sems):
        if count == 1:
            return

        @pl.when(index > 0)
        def _():
            pl.semaphore_wait(chain_sem.at[sems], 1)

        @pl.when(index < count - 1)
        def _():
            notify(chain_sem.at[sems], up)
            pl.semaphore_wait(chain_sem.at[sems + 1], 1)

        @pl.when(index > 0)
        def _():
            notify(chain_sem.at[sems + 1], down)

    chain(near["y+"], near["y-"], ny, iy, 0)
    chain(near["z+"], near["z-"], nz, iz, 2)
    for d in range(1, nx):
        notify(chain_sem.at[4], at(x=lax.rem(ix + d, nx)))

    lane = lax.broadcasted_iota(jnp.int32, (1, bz), 1)
    group = lane // SEG
    spot = lax.rem(lane, SEG)

    def pack(read, k):
        acc = None
        for g in range(groups):
            x = tiles * g + k
            if x >= win:
                continue
            moved = roll(read(x), H + SEG * g)
            acc = moved if acc is None else jnp.where(group == g, moved, acc)
        return acc

    def prepare(f, field):
        for x in range(win):
            tile = field[x]
            ys[0, f, x * H : x * H + H] = tile[by - H : by]
            ys[1, f, x * H : x * H + H] = tile[0:H]
        for k in range(tiles):
            tile = pack(lambda x: field[x], k)
            ss[f, k] = tile
            ds[0, f, k * H : k * H + H] = tile[by - H : by]
            ds[1, f, k * H : k * H + H] = tile[0:H]

    both = lambda a, b: jnp.logical_and(has[a], has[b])

    def exchange(f):
        def send(src, dst, n, device):
            return pltpu.make_async_remote_copy(
                src_ref=src.at[f],
                dst_ref=dst.at[f],
                send_sem=hs_sem.at[f, n],
                recv_sem=hr_sem.at[f, n],
                device_id=device,
                device_id_type=MESH,
            )

        up, down = ds.at[0], ds.at[1]
        pp, pm = both("y+", "z+"), both("y+", "z-")
        mp, mm = both("y-", "z+"), both("y-", "z-")
        return [
            (send(ys.at[0], yr.at[0], 0, near["y+"]), has["y+"], has["y-"]),
            (send(ys.at[1], yr.at[1], 1, near["y-"]), has["y-"], has["y+"]),
            (send(ss, zr.at[0], 2, near["z+"]), has["z+"], has["z-"]),
            (send(ss, zr.at[1], 3, near["z-"]), has["z-"], has["z+"]),
            (send(up, dr.at[0], 4, at(y=iy + 1, z=iz + 1)), pp, mm),
            (send(up, dr.at[1], 5, at(y=iy + 1, z=iz - 1)), pm, mp),
            (send(down, dr.at[2], 6, at(y=iy - 1, z=iz + 1)), mp, pm),
            (send(down, dr.at[3], 7, at(y=iy - 1, z=iz - 1)), mm, pp),
        ]

    def send_all(f):
        for copy, sends, _ in exchange(f):
            pl.when(sends)(copy.start)

    def receive_all(f):
        for copy, _, receives in exchange(f):
            pl.when(receives)(copy.wait_recv)

    front = 8

    def base(x):
        return front + x * yp

    def assemble(f, field, whole):
        for x in range(win):
            b = base(x)
            whole[b + H : b + H + by] = field[x]
            whole[b : b + H] = yr[0, f, x * H : x * H + H]
            whole[b + H + by : b + 2 * H + by] = yr[1, f, x * H : x * H + H]
        for k in range(tiles):
            for z in range(2):
                za[z, H : H + by] = zr[z, f, k]
                za[z, 0:H] = dr[z, f, k * H : k * H + H]
                za[z, H + by : 2 * H + by] = dr[2 + z, f, k * H : k * H + H]
            left = za[0, 0:yp]
            mine = pack(lambda x: whole[base(x) : base(x) + yp], k)
            right = roll(za[1, 0:yp], SEG // 2)
            b = base(win + k)
            whole[b : b + yp] = jnp.where(
                spot < H,
                left,
                jnp.where(
                    spot < SEG // 2,
                    mine,
                    jnp.where(spot < SEG // 2 + H, roll(mine, SEG // 2), right),
                ),
            )

    if nx > 1:
        for side in range(2):
            zone = vw.at[pl.ds(off - H if side == 0 else off + bx, H)]
            arrived = pltpu.make_async_copy(zone, zone, vr_sem.at[side])
            pl.when(ix > 0 if side == 0 else ix < nx - 1)(arrived.wait)
    prepare(0, vw)
    send_all(0)

    squares = jnp.zeros((by, bz), jnp.float32)
    for p in range(PIECES):
        for d in range(1, nx):
            x_copy(d, p).wait_recv()
        for r in range(p * size, (p + 1) * size):
            row = psum[ix * bx + r]
            for d in range(1, nx):
                row = row + xr[d - 1, r]
            gw[off + r] = row
            squares = squares + row * row
    count = nx * ny * nz
    me = (ix * ny + iy) * nz + iz
    ar[me] = jnp.sum(squares, axis=0, keepdims=True)
    if nx > 1:
        pl.semaphore_wait(chain_sem.at[4], nx - 1)

    def send_square(d, carry):
        other = lax.rem(me + d, count)
        pltpu.make_async_remote_copy(
            src_ref=ar.at[me],
            dst_ref=ar.at[me],
            send_sem=ars_sem,
            recv_sem=arr_sem,
            device_id=(other // (ny * nz), lax.rem(other // nz, ny), lax.rem(other, nz)),
            device_id_type=MESH,
        ).start()
        return carry

    if count <= 64:
        for d in range(count - 1, 0, -1):
            send_square(d, 0)
    else:
        lax.fori_loop(1, count, send_square, 0)

    for side in range(2):
        if nx == 1:
            break
        present = ix > 0 if side == 0 else ix < nx - 1

        @pl.when(present)
        def _(side=side):
            for d in range(1, nx):
                zone = xh.at[d - 1, side]
                pltpu.make_async_copy(zone, zone, xhr_sem.at[d - 1, side]).wait()
            for r in range(H):
                there = ix * bx - H + r if side == 0 else ix * bx + bx + r
                row = psum[there]
                for d in range(1, nx):
                    row = row + xh[d - 1, side, r]
                gw[(off - H if side == 0 else off + bx) + r] = row

    prepare(1, gw)
    send_all(1)
    receive_all(0)
    assemble(0, vw, va)
    receive_all(1)
    assemble(1, gw, ga)

    many = ar.at[pl.ds(0, count - 1)]
    pltpu.make_async_copy(many, many, arr_sem).wait()
    square_sum = jnp.sum(jnp.sum(ar[...], axis=0), axis=1, keepdims=True)
    cells = nx * ny * nz * bx * by * bz
    scale = step_length * lax.rsqrt(square_sum / cells + 1.0)

    scale_out[...] = jnp.broadcast_to(scale, scale_out.shape)

    for d in range(1, nx):
        for p in range(PIECES):
            x_copy(d, p).wait_send()
        q = lax.rem(ix + d, nx)
        pl.when(q > 0)(halo_copy(d, 0).wait_send)
        pl.when(q < nx - 1)(halo_copy(d, 1).wait_send)
    if nx > 1:
        pl.when(ix < nx - 1)(v_halo(0).wait_send)
        pl.when(ix > 0)(v_halo(1).wait_send)
    for f in range(2):
        for copy, sends, _ in exchange(f):
            pl.when(sends)(copy.wait_send)
    pltpu.make_async_copy(many, many, ars_sem).wait()


def proximal(
    dims,
    va,
    ga,
    gw,
    scale_in,
    gradient_out,
    model_out,
    target,
    current,
    extra,
    dx,
    dy,
    dz,
    result,
    out_sem,
):
    nx, ny, nz, slots, bx, by, bz = dims
    win, tiles, yp, flat = geometry(dims)
    ix, iy, iz = lax.axis_index("gx"), lax.axis_index("gy"), lax.axis_index("gz")
    off = own_offset(nx, bx, win, ix)
    g_out = pltpu.make_async_copy(gw.at[pl.ds(off, bx)], gradient_out, out_sem.at[0])
    g_out.start()
    front = 8

    def base(x):
        return front + x * yp

    edge_rows = jnp.zeros((front, bz), jnp.float32)
    dy[0:front] = edge_rows
    target[flat - front : flat] = edge_rows
    extra[flat - front : flat] = edge_rows
    scale = scale_in[...]
    lane = lax.broadcasted_iota(jnp.int32, (1, bz), 1)
    group = lane // SEG
    spot = lax.rem(lane, SEG)
    y_at = iy * by - H + lax.broadcasted_iota(jnp.int32, (yp, 1), 0)
    keep_y = jnp.logical_and(y_at >= 0, y_at < ny * by - 1)
    keep_y = jnp.broadcast_to(keep_y, (yp, bz))
    z_main = iz * bz + lane
    keep_z_main = jnp.broadcast_to(z_main < nz * bz - 1, (yp, bz))
    z_pack = iz * bz + jnp.where(spot < SEG // 2, spot - H, spot - SEG // 2 + bz - H)
    keep_z_pack = jnp.broadcast_to(
        jnp.logical_and(z_pack >= 0, z_pack < nz * bz - 1), (yp, bz)
    )
    start = ix * bx - off
    blocks = win + tiles

    def rows(ref, x, shift=0):
        return ref[base(x) + shift : base(x) + shift + yp]

    for x in range(blocks):
        value = rows(va, x) - scale * rows(ga, x)
        target[base(x) : base(x) + yp] = value

    for it in range(ITERS):
        now = target if it == 0 else extra
        held = target if it == 0 else current
        last = it == ITERS - 1
        for x in range(blocks):
            here = rows(now, x)
            b = base(x)
            ddy = jnp.where(keep_y, rows(now, x, 1) - here, 0.0)
            if x < win:
                g, k = x // tiles, x % tiles
                edge = roll(rows(now, win + k), bz - 1 - (SEG * g + SEG // 2 + H))
                after = jnp.where(lane == bz - 1, edge, roll(here, -1))
                ddz = jnp.where(keep_z_main, after - here, 0.0)
                if x == win - 1:
                    ddx = jnp.zeros_like(here)
                else:
                    ddx = rows(now, x + 1) - here
            else:
                k = x - win
                ddz = jnp.where(keep_z_pack, roll(here, -1) - here, 0.0)
                if k < tiles - 1:
                    after = rows(now, x + 1)
                else:
                    after = roll(rows(now, win), -SEG)
                ddx = jnp.where(tiles * group + k < win - 1, after - here, 0.0)
            px, py, pz = dual_step * ddx, dual_step * ddy, dual_step * ddz
            if it > 0:
                px, py, pz = rows(dx, x) + px, rows(dy, x) + py, rows(dz, x) + pz
            shrink = jnp.minimum(1.0, tv_weight * lax.rsqrt(px * px + py * py + pz * pz))
            dx[b : b + yp] = px * shrink
            dy[b : b + yp] = py * shrink
            dz[b : b + yp] = pz * shrink
        for x in range(win if last else blocks):
            b = base(x)
            qx, qy, qz = rows(dx, x), rows(dy, x), rows(dz, x)
            spread = qy - rows(dy, x, -1)
            if x < win:
                g, k = x // tiles, x % tiles
                edge = roll(rows(dz, win + k), -(SEG * g + H - 1))
                spread = spread + (qz - jnp.where(lane == 0, edge, roll(qz, 1)))
                spread = spread + (qx if x == 0 else qx - rows(dx, x - 1))
            else:
                k = x - win
                spread = spread + (qz - roll(qz, 1))
                before = rows(dx, x - 1) if k > 0 else roll(rows(dx, blocks - 1), SEG)
                spread = spread + (qx - before)
            old = rows(held, x)
            new = (old + primal_step * (spread + rows(target, x))) * (1.0 / (1.0 + primal_step))
            if last:
                result[x] = new[H : H + by]
            else:
                current[b : b + yp] = new
                extra[b : b + yp] = 2.0 * new - old

    m_out = pltpu.make_async_copy(result.at[pl.ds(off, bx)], model_out, out_sem.at[1])
    m_out.start()
    g_out.wait()
    m_out.wait()


def shards(partials, code_bits, group_map, velocity):
    slots = partials.shape[0]
    bx, by, bz = velocity.shape
    nx, ny, nz = (lax.axis_size(a) for a in ("gx", "gy", "gz"))
    dims = (nx, ny, nz, slots, bx, by, bz)
    win, tiles, yp, flat = geometry(dims)
    strip = -(-(win * H + 5) // 8) * 8
    diag = -(-(tiles * H + 5) // 8) * 8
    f32 = functools.partial(pltpu.VMEM, dtype=jnp.float32)
    peers = max(nx - 1, 1)
    dma = pltpu.SemaphoreType.DMA
    anywhere = pl.BlockSpec(memory_space=pl.ANY)
    near = pl.BlockSpec(memory_space=pltpu.VMEM)
    block = jax.ShapeDtypeStruct(velocity.shape, jnp.float32)
    handed = (f32((flat, bz)), f32((flat, bz)), f32((win, by, bz)), f32((1, bz)))
    assembled = pl.pallas_call(
        functools.partial(kernel, dims),
        out_shape=handed,
        in_specs=[pl.BlockSpec(memory_space=pltpu.HBM)] * 4,
        out_specs=(near,) * 4,
        scratch_shapes=[
            pltpu.SMEM(code_bits.shape, jnp.int32),
            pltpu.SMEM(group_map.shape, jnp.int32),
            f32(partials.shape),
            f32((nx * bx, by, bz)),
            f32((win, by, bz)),
            f32((peers, bx, by, bz)),
            f32((peers, 2, H, by, bz)),
            f32((2, 2, strip, bz)),
            f32((2, 2, strip, bz)),
            f32((2, tiles, by, bz)),
            f32((2, 2, tiles, by, bz)),
            f32((2, 2, diag, bz)),
            f32((4, 2, diag, bz)),
            f32((2, yp + 8, bz)),
            f32((nx * ny * nz, 1, bz)),
            dma((3,)),
            dma((nx * PIECES,)),
            dma((peers, PIECES)),
            dma((peers, PIECES)),
            dma((peers, 2)),
            dma((peers, 2)),
            dma((2,)),
            dma((2,)),
            dma((2, 8)),
            dma((2, 8)),
            dma,
            dma,
            pltpu.SemaphoreType.REGULAR((5,)),
        ],
        compiler_params=pltpu.CompilerParams(
            collective_id=0, has_side_effects=True
        ),
    )(partials, code_bits, group_map, velocity)
    return pl.pallas_call(
        functools.partial(proximal, dims),
        out_shape=(block, block),
        in_specs=[near] * 4,
        out_specs=(anywhere, anywhere),
        scratch_shapes=[f32((flat, bz))] * 6 + [f32((win, by, bz)), dma((2,))],
        compiler_params=pltpu.CompilerParams(vmem_limit_bytes=32 * 2**20),
    )(*assembled)


def solution(mesh):
    placed = (P("gx", None, "gy", "gz"), P(), P(), P("gx", "gy", "gz"))
    return jax.shard_map(
        shards,
        mesh=mesh,
        in_specs=placed,
        out_specs=(P("gx", "gy", "gz"), P("gx", "gy", "gz")),
        check_vma=False,
    )
```

profile of v0, /device:TPU:1, one launch (start us, length us, event | category | flops | bytes accessed | tf_op | source)
XLA Modules:
  0.0 41.8 jit_solution(6742761667485328069)
XLA Ops:
  0.6 39.1 %shard_map.59 = (f32[616,128]{1,0:T(8,128)S(1)}, f32[616,128]{1,0:T(8,128)S(1)}, f32[22,16,128]{2,1,0:T(8,128)S(1)}, f32[1,128]{1,0:T(1,128)S(1)}) custom-call(f32[4,128,16,128]{3,2,1,0:T(8,128)} %partials.1, s32[32,128]{1,0:T(8,128)} %code_bits.1, s32[32]{0:T(128)} %group_map.1, f32[16,16,128]{2,1,0:T(8,128)} %velocity.1), custom_call_target="tpu_custom_call" | custom-call | tf_op jit(solution)/shard_map/pallas_call | solution.py:556
  39.7 2.1 %shard_map.60 = (f32[16,16,128]{2,1,0:T(8,128)}, f32[16,16,128]{2,1,0:T(8,128)}) custom-call(f32[616,128]{1,0:T(8,128)S(1)} %get-tuple-element.6.va, f32[616,128]{1,0:T(8,128)S(1)} %get-tuple-element.7.ga, f32[22,16,128]{2,1,0:T(8,128)S(1)} %get-tuple-element.8.gw, f32[1,128]{1,0:T(1,128)S(1)} %get-tuple-element.9.scale_in), custom_call_target="tpu_custom_call" | custom-call | tf_op jit(solution)/shard_map/pallas_call | solution.py:595
where the time goes:
time: 41.9 us; the launch traced here: 41.8 us
  Pallas kernels  41.1 us (98%)
  between operations  0.64 us (2%)
    pallas_call x1, Pallas kernels, shards(): pl.pallas_call(functools.partial(kernel, dims), out_shape=handed, in_spec...  39.1 us
    pallas_call x1, Pallas kernels, shards(): pl.pallas_call(functools.partial(proximal, dims), out_shape=(block, block...  2.07 us

commit v1 on v0

--- a/solution.py
+++ b/solution.py
@@ -10,7 +10,8 @@
 ITERS = 3
 H = ITERS
 SEG = 16
-PIECES = 4
+PARTS = ((2, 6, 1), (6, 1, 2), (1, 2, 6))
+LOAD_ORDER = (5, 4, 7, 3, 2, 6, 1, 0)
 
 step_length = 0.5
 tv_weight = 0.2
@@ -36,6 +37,17 @@
 def roll(value, shift):
     shift = shift % value.shape[1]
     return value if shift == 0 else pltpu.roll(value, shift, 1)
+
+
+def xor_masks(ix):
+    two = ix + 2 - 4 * lax.rem(lax.div(ix, 2), 2)
+    six = 6 - 2 * lax.div(ix, 2) + lax.rem(ix, 2)
+    four = lax.rem(ix + 4, 8)
+    flip = lambda q: q + 1 - 2 * lax.rem(q, 2)
+    return {
+        0: ix, 1: flip(ix), 2: two, 3: flip(two),
+        4: four, 5: flip(four), 6: six, 7: flip(six),
+    }
 
 
 def kernel(
@@ -53,8 +65,11 @@
     part,
     psum,
     vw,
-    xr,
-    xh,
+    r1,
+    r2,
+    r3,
+    s2,
+    s3,
     ys,
     yr,
     ss,
@@ -62,32 +77,34 @@
     ds,
     dr,
     za,
-    ar,
+    ara,
+    arb,
     in_sem,
     part_sem,
+    s1_sems,
+    r1_sems,
+    s2_sems,
+    r2_sems,
+    s3_sems,
+    r3_sems,
     xs_sem,
     xr_sem,
-    xhs_sem,
-    xhr_sem,
-    vs_sem,
-    vr_sem,
     hs_sem,
     hr_sem,
-    ars_sem,
-    arr_sem,
-    chain_sem,
+    as_sem,
+    ar_sem,
+    bs_sem,
+    br_sem,
 ):
     nx, ny, nz, slots, bx, by, bz = dims
     win, tiles, yp, flat = geometry(dims)
     groups = bz // SEG
     ix, iy, iz = lax.axis_index("gx"), lax.axis_index("gy"), lax.axis_index("gz")
+    xi, zl = lax.div(ix, 2), lax.rem(ix, 2)
     offset = functools.partial(own_offset, nx, bx, win)
     off = offset(ix)
-    size = bx // PIECES
-    order = [(d, p) for d in list(range(1, nx)) + [0] for p in range(PIECES)]
-
-    def first_row(d, p):
-        return lax.rem(ix + d, nx) * bx + p * size
+    block = xor_masks(ix)
+    per = bx * by // 8
 
     in_copies = [
         pltpu.make_async_copy(code_bits, bits, in_sem.at[0]),
@@ -96,15 +113,14 @@
     v_copy = pltpu.make_async_copy(velocity, vw.at[pl.ds(off, bx)], in_sem.at[2])
     for c in in_copies:
         c.start()
+    part_copies = {}
+    for mask in LOAD_ORDER:
+        where = pl.ds(block[mask] * bx, bx)
+        part_copies[mask] = pltpu.make_async_copy(
+            partials.at[:, where], part.at[:, where], part_sem.at[mask]
+        )
+        part_copies[mask].start()
     v_copy.start()
-    part_copies = []
-    for n, (d, p) in enumerate(order):
-        where = pl.ds(first_row(d, p), size)
-        part_copies.append(
-            pltpu.make_async_copy(partials.at[:, where], part.at[:, where], part_sem.at[n])
-        )
-    for c in part_copies:
-        c.start()
 
     barrier = pltpu.get_barrier_semaphore()
 
@@ -117,8 +133,18 @@
     for buffer in (yr, zr, dr):
         buffer[...] = jnp.zeros_like(buffer)
 
-    for d in range(1, nx):
-        notify(barrier, at(x=lax.rem(ix + d, nx)))
+    ring = lambda d, n: min(d, n - d)
+    plane = [(dx, dz) for dx in range(4) for dz in range(nz) if dx or dz]
+    plane.sort(key=lambda p: -(ring(p[0], 4) + ring(p[1], nz)))
+    stack = [(dl, dy) for dl in range(2) for dy in range(ny) if dl or dy]
+    stack.sort(key=lambda p: -(p[0] + 2 * ring(p[1] // 2, max(ny // 2, 1)) + p[1] % 2))
+
+    def plane_device(dx, dz):
+        return at(x=2 * lax.rem(xi + dx, 4) + zl, z=lax.rem(iz + dz, nz))
+
+    def stack_device(dl, dy):
+        return at(x=2 * xi + lax.rem(zl + dl, 2), y=lax.rem(iy + dy, ny))
+
     has = {
         "y-": iy > 0,
         "y+": iy < ny - 1,
@@ -131,46 +157,61 @@
         "z-": at(z=iz - 1),
         "z+": at(z=iz + 1),
     }
-    total = jnp.int32(nx - 1)
-    for key in has:
-        total = total + has[key].astype(jnp.int32)
-
-        @pl.when(has[key])
-        def _(key=key):
-            notify(barrier, near[key])
+    both = lambda a, b: jnp.logical_and(has[a], has[b])
+    for p in plane:
+        notify(barrier, plane_device(*p))
+    for p in stack:
+        notify(barrier, stack_device(*p))
+    total = jnp.int32(len(plane) + len(stack))
+    extra = [
+        (both("y+", "z+"), at(y=iy + 1, z=iz + 1)),
+        (both("y+", "z-"), at(y=iy + 1, z=iz - 1)),
+        (both("y-", "z+"), at(y=iy - 1, z=iz + 1)),
+        (both("y-", "z-"), at(y=iy - 1, z=iz - 1)),
+        (jnp.logical_and(zl == 1, ix < nx - 1), at(x=ix + 1)),
+        (jnp.logical_and(zl == 0, ix > 0), at(x=ix - 1)),
+    ]
+    for present, device in extra:
+        total = total + present.astype(jnp.int32)
+
+        @pl.when(present)
+        def _(device=device):
+            notify(barrier, device)
 
     for buffer in (za, va, ga):
         buffer[...] = jnp.zeros_like(buffer)
-    pl.semaphore_wait(barrier, total)
-
-    def v_halo(side):
+
+    def x_halo(buffer, f, side):
         q = ix + 1 if side == 0 else ix - 1
         src = off + bx - H if side == 0 else off
         dst = offset(q) - H if side == 0 else offset(q) + bx
         return pltpu.make_async_remote_copy(
-            src_ref=vw.at[pl.ds(src, H)],
-            dst_ref=vw.at[pl.ds(dst, H)],
-            send_sem=vs_sem.at[side],
-            recv_sem=vr_sem.at[side],
+            src_ref=buffer.at[pl.ds(src, H)],
+            dst_ref=buffer.at[pl.ds(dst, H)],
+            send_sem=xs_sem.at[f, side],
+            recv_sem=xr_sem.at[f, side],
             device_id=at(x=q),
             device_id_type=MESH,
         )
 
-    v_copy.wait()
-    if nx > 1:
-        @pl.when(ix < nx - 1)
-        def _():
-            v_halo(0).start()
-
-        @pl.when(ix > 0)
-        def _():
-            v_halo(1).start()
+    def x_send(buffer, f):
+        pl.when(ix < nx - 1)(x_halo(buffer, f, 0).start)
+        pl.when(ix > 0)(x_halo(buffer, f, 1).start)
+
+    def x_arrive(buffer, f):
+        for side in range(2):
+            zone = buffer.at[pl.ds(off - H if side == 0 else off + bx, H)]
+            arrived = pltpu.make_async_copy(zone, zone, xr_sem.at[f, side])
+            pl.when(ix > 0 if side == 0 else ix < nx - 1)(arrived.wait)
 
     for c in in_copies:
         c.wait()
     codes = [gmap[ix * slots + s] for s in range(slots)]
 
-    def reduce_rows(first):
+    def reduce_block(mask):
+        part_copies[mask].wait()
+        first = block[mask] * bx
+
         def one(r, carry):
             row = first + r
             acc = None
@@ -178,71 +219,57 @@
                 sign = (2 * bits[codes[s], row] - 1).astype(jnp.float32)
                 term = sign * part[s, row]
                 acc = term if acc is None else acc + term
-            psum[row] = acc
+            for h in range(by // 8):
+                psum[row * (by // 8) + h] = acc[8 * h : 8 * h + 8]
             return carry
 
-        lax.fori_loop(0, size, one, 0, unroll=2)
-
-    def x_copy(d, p):
+        lax.fori_loop(0, bx, one, 0, unroll=4)
+
+    cuts = [per * k // 3 for k in range(4)]
+
+    def span(mask, k):
+        return pl.ds(block[mask] * per + cuts[k], cuts[k + 1] - cuts[k])
+
+    def hop(k, step, m, src):
+        width = cuts[k + 1] - cuts[k]
+        to = r1.at[k, m] if step == 0 else r2.at[k, m] if step == 1 else r3.at[k]
+        sends = s1_sems.at[k, m] if step == 0 else s2_sems.at[k, m] if step == 1 else s3_sems.at[k]
+        recvs = r1_sems.at[k, m] if step == 0 else r2_sems.at[k, m] if step == 1 else r3_sems.at[k]
         return pltpu.make_async_remote_copy(
-            src_ref=psum.at[pl.ds(first_row(d, p), size)],
-            dst_ref=xr.at[d - 1, pl.ds(p * size, size)],
-            send_sem=xs_sem.at[d - 1, p],
-            recv_sem=xr_sem.at[d - 1, p],
-            device_id=at(x=lax.rem(ix + d, nx)),
+            src_ref=src,
+            dst_ref=to.at[pl.ds(0, width)],
+            send_sem=sends,
+            recv_sem=recvs,
+            device_id=at(x=block[PARTS[k][step]]),
             device_id_type=MESH,
         )
 
-    for n, (d, p) in enumerate(order):
-        part_copies[n].wait()
-        reduce_rows(first_row(d, p))
-        if d > 0:
-            x_copy(d, p).start()
-
-    def halo_copy(d, side):
-        q = lax.rem(ix + d, nx)
-        first = q * bx - H if side == 0 else q * bx + bx
-        return pltpu.make_async_remote_copy(
-            src_ref=psum.at[pl.ds(first, H)],
-            dst_ref=xh.at[d - 1, side],
-            send_sem=xhs_sem.at[d - 1, side],
-            recv_sem=xhr_sem.at[d - 1, side],
-            device_id=at(x=q),
-            device_id_type=MESH,
-        )
-
-    for d in range(1, nx):
-        q = lax.rem(ix + d, nx)
-
-        @pl.when(q > 0)
-        def _(d=d):
-            halo_copy(d, 0).start()
-
-        @pl.when(q < nx - 1)
-        def _(d=d):
-            halo_copy(d, 1).start()
-
-    def chain(up, down, count, index, sems):
-        if count == 1:
-            return
-
-        @pl.when(index > 0)
-        def _():
-            pl.semaphore_wait(chain_sem.at[sems], 1)
-
-        @pl.when(index < count - 1)
-        def _():
-            notify(chain_sem.at[sems], up)
-            pl.semaphore_wait(chain_sem.at[sems + 1], 1)
-
-        @pl.when(index > 0)
-        def _():
-            notify(chain_sem.at[sems + 1], down)
-
-    chain(near["y+"], near["y-"], ny, iy, 0)
-    chain(near["z+"], near["z-"], nz, iz, 2)
-    for d in range(1, nx):
-        notify(chain_sem.at[4], at(x=lax.rem(ix + d, nx)))
+    def kept(k):
+        a, b, c = PARTS[k]
+        return [b ^ c, b, c, 0]
+
+    def first_hop(k, m):
+        return hop(k, 0, m, psum.at[span(PARTS[k][0] ^ kept(k)[m], k)])
+
+    def second_hop(k, m):
+        return hop(k, 1, m, s2.at[k, m, pl.ds(0, cuts[k + 1] - cuts[k])])
+
+    def third_hop(k):
+        return hop(k, 2, 0, s3.at[k, pl.ds(0, cuts[k + 1] - cuts[k])])
+
+    done = set()
+    for m in range(4):
+        for k in range(3):
+            mask = PARTS[k][0] ^ kept(k)[m]
+            if mask not in done:
+                done.add(mask)
+                reduce_block(mask)
+                if len(done) == 1:
+                    pl.semaphore_wait(barrier, total)
+            first_hop(k, m).start()
+    reduce_block(0)
+    v_copy.wait()
+    x_send(vw, 0)
 
     lane = lax.broadcasted_iota(jnp.int32, (1, bz), 1)
     group = lane // SEG
@@ -268,8 +295,6 @@
             ss[f, k] = tile
             ds[0, f, k * H : k * H + H] = tile[by - H : by]
             ds[1, f, k * H : k * H + H] = tile[0:H]
-
-    both = lambda a, b: jnp.logical_and(has[a], has[b])
 
     def exchange(f):
         def send(src, dst, n, device):
@@ -334,93 +359,88 @@
                 ),
             )
 
-    if nx > 1:
-        for side in range(2):
-            zone = vw.at[pl.ds(off - H if side == 0 else off + bx, H)]
-            arrived = pltpu.make_async_copy(zone, zone, vr_sem.at[side])
-            pl.when(ix > 0 if side == 0 else ix < nx - 1)(arrived.wait)
+    for m in range(2):
+        for k in range(3):
+            first_hop(k, m).wait_recv()
+            width = cuts[k + 1] - cuts[k]
+            s2[k, m, 0:width] = psum[span(kept(k)[m], k)] + r1[k, m, 0:width]
+            second_hop(k, m).start()
+
+    x_arrive(vw, 0)
     prepare(0, vw)
     send_all(0)
 
-    squares = jnp.zeros((by, bz), jnp.float32)
-    for p in range(PIECES):
-        for d in range(1, nx):
-            x_copy(d, p).wait_recv()
-        for r in range(p * size, (p + 1) * size):
-            row = psum[ix * bx + r]
-            for d in range(1, nx):
-                row = row + xr[d - 1, r]
-            gw[off + r] = row
-            squares = squares + row * row
-    count = nx * ny * nz
-    me = (ix * ny + iy) * nz + iz
-    ar[me] = jnp.sum(squares, axis=0, keepdims=True)
-    if nx > 1:
-        pl.semaphore_wait(chain_sem.at[4], nx - 1)
-
-    def send_square(d, carry):
-        other = lax.rem(me + d, count)
-        pltpu.make_async_remote_copy(
-            src_ref=ar.at[me],
-            dst_ref=ar.at[me],
-            send_sem=ars_sem,
-            recv_sem=arr_sem,
-            device_id=(other // (ny * nz), lax.rem(other // nz, ny), lax.rem(other, nz)),
-            device_id_type=MESH,
-        ).start()
-        return carry
-
-    if count <= 64:
-        for d in range(count - 1, 0, -1):
-            send_square(d, 0)
-    else:
-        lax.fori_loop(1, count, send_square, 0)
-
-    for side in range(2):
-        if nx == 1:
-            break
-        present = ix > 0 if side == 0 else ix < nx - 1
-
-        @pl.when(present)
-        def _(side=side):
-            for d in range(1, nx):
-                zone = xh.at[d - 1, side]
-                pltpu.make_async_copy(zone, zone, xhr_sem.at[d - 1, side]).wait()
-            for r in range(H):
-                there = ix * bx - H + r if side == 0 else ix * bx + bx + r
-                row = psum[there]
-                for d in range(1, nx):
-                    row = row + xh[d - 1, side, r]
-                gw[(off - H if side == 0 else off + bx) + r] = row
-
+    for k in range(3):
+        first_hop(k, 2).wait_recv()
+        second_hop(k, 0).wait_recv()
+        width = cuts[k + 1] - cuts[k]
+        mine = psum[span(kept(k)[2], k)] + r1[k, 2, 0:width]
+        s3[k, 0:width] = mine + r2[k, 0, 0:width]
+        third_hop(k).start()
+
+    squares = jnp.zeros((8, bz), jnp.float32)
+    for k in range(3):
+        first_hop(k, 3).wait_recv()
+        second_hop(k, 1).wait_recv()
+        third_hop(k).wait_recv()
+        for j in range(cuts[k], cuts[k + 1]):
+            n = j - cuts[k]
+            value = psum[ix * per + j] + r1[k, 3, n] + (r2[k, 1, n] + r3[k, n])
+            r, h = divmod(j, by // 8)
+            gw[off + r, 8 * h : 8 * h + 8] = value
+            squares = squares + value * value
+
+    def spread(buffer, me, peers, device, send_sem, recv_sem):
+        for p in peers:
+            pltpu.make_async_remote_copy(
+                src_ref=buffer.at[me],
+                dst_ref=buffer.at[me],
+                send_sem=send_sem,
+                recv_sem=recv_sem,
+                device_id=device(*p),
+                device_id_type=MESH,
+            ).start()
+
+    def drain(buffer, peers, sem):
+        many = buffer.at[pl.ds(0, len(peers))]
+        pltpu.make_async_copy(many, many, sem).wait()
+
+    me_a = xi * nz + iz
+    ara[me_a] = jnp.sum(squares, axis=0, keepdims=True)
+    spread(ara, me_a, plane, plane_device, as_sem, ar_sem)
+    x_send(gw, 1)
+    receive_all(0)
+    assemble(0, vw, va)
+    for k in range(3):
+        for m in range(4):
+            first_hop(k, m).wait_send()
+        for m in range(2):
+            second_hop(k, m).wait_send()
+        third_hop(k).wait_send()
+    x_arrive(gw, 1)
     prepare(1, gw)
     send_all(1)
-    receive_all(0)
-    assemble(0, vw, va)
+
+    drain(ara, plane, ar_sem)
+    me_b = zl * ny + iy
+    arb[me_b] = jnp.sum(ara[...], axis=0)
+    spread(arb, me_b, stack, stack_device, bs_sem, br_sem)
+
     receive_all(1)
     assemble(1, gw, ga)
-
-    many = ar.at[pl.ds(0, count - 1)]
-    pltpu.make_async_copy(many, many, arr_sem).wait()
-    square_sum = jnp.sum(jnp.sum(ar[...], axis=0), axis=1, keepdims=True)
+    drain(ara, plane, as_sem)
+    for f, buffer in ((0, vw), (1, gw)):
+        pl.when(ix < nx - 1)(x_halo(buffer, f, 0).wait_send)
+        pl.when(ix > 0)(x_halo(buffer, f, 1).wait_send)
+        for copy, sends, _ in exchange(f):
+            pl.when(sends)(copy.wait_send)
+
+    drain(arb, stack, br_sem)
+    square_sum = jnp.sum(jnp.sum(arb[...], axis=0), axis=1, keepdims=True)
     cells = nx * ny * nz * bx * by * bz
     scale = step_length * lax.rsqrt(square_sum / cells + 1.0)
-
     scale_out[...] = jnp.broadcast_to(scale, scale_out.shape)
-
-    for d in range(1, nx):
-        for p in range(PIECES):
-            x_copy(d, p).wait_send()
-        q = lax.rem(ix + d, nx)
-        pl.when(q > 0)(halo_copy(d, 0).wait_send)
-        pl.when(q < nx - 1)(halo_copy(d, 1).wait_send)
-    if nx > 1:
-        pl.when(ix < nx - 1)(v_halo(0).wait_send)
-        pl.when(ix > 0)(v_halo(1).wait_send)
-    for f in range(2):
-        for copy, sends, _ in exchange(f):
-            pl.when(sends)(copy.wait_send)
-    pltpu.make_async_copy(many, many, ars_sem).wait()
+    drain(arb, stack, bs_sem)
 
 
 def proximal(
@@ -547,7 +567,8 @@
     strip = -(-(win * H + 5) // 8) * 8
     diag = -(-(tiles * H + 5) // 8) * 8
     f32 = functools.partial(pltpu.VMEM, dtype=jnp.float32)
-    peers = max(nx - 1, 1)
+    per = bx * by // 8
+    third = -(-per // 3)
     dma = pltpu.SemaphoreType.DMA
     anywhere = pl.BlockSpec(memory_space=pl.ANY)
     near = pl.BlockSpec(memory_space=pltpu.VMEM)
@@ -562,10 +583,13 @@
             pltpu.SMEM(code_bits.shape, jnp.int32),
             pltpu.SMEM(group_map.shape, jnp.int32),
             f32(partials.shape),
-            f32((nx * bx, by, bz)),
+            f32((nx * per, 8, bz)),
             f32((win, by, bz)),
-            f32((peers, bx, by, bz)),
-            f32((peers, 2, H, by, bz)),
+            f32((3, 4, third, 8, bz)),
+            f32((3, 2, third, 8, bz)),
+            f32((3, third, 8, bz)),
+            f32((3, 2, third, 8, bz)),
+            f32((3, third, 8, bz)),
             f32((2, 2, strip, bz)),
             f32((2, 2, strip, bz)),
             f32((2, tiles, by, bz)),
@@ -573,20 +597,24 @@
             f32((2, 2, diag, bz)),
             f32((4, 2, diag, bz)),
             f32((2, yp + 8, bz)),
-            f32((nx * ny * nz, 1, bz)),
+            f32((4 * nz, 1, bz)),
+            f32((2 * ny, 1, bz)),
             dma((3,)),
-            dma((nx * PIECES,)),
-            dma((peers, PIECES)),
-            dma((peers, PIECES)),
-            dma((peers, 2)),
-            dma((peers, 2)),
-            dma((2,)),
-            dma((2,)),
+            dma((nx,)),
+            dma((3, 4)),
+            dma((3, 4)),
+            dma((3, 2)),
+            dma((3, 2)),
+            dma((3,)),
+            dma((3,)),
+            dma((2, 2)),
+            dma((2, 2)),
             dma((2, 8)),
             dma((2, 8)),
             dma,
             dma,
-            pltpu.SemaphoreType.REGULAR((5,)),
+            dma,
+            dma,
         ],
         compiler_params=pltpu.CompilerParams(
             collective_id=0, has_side_effects=True

time: 41.9 us -> 35.3 us (0.84)
  Pallas kernels: 41.1 us -> 34.6 us
    pallas_call x1, Pallas kernels: 39.1 us -> 32.6 us  [shards(): pl.pallas_call(functools.partial(kernel, dims), out_shape=handed, in_spec...]
where the time goes in v1:
time: 35.3 us
  Pallas kernels  34.6 us (98%)
  between operations  0.64 us (2%)
    pallas_call x1, Pallas kernels, shards(): pl.pallas_call(functools.partial(kernel, dims), out_shape=handed, in_spec...  32.6 us
    pallas_call x1, Pallas kernels, shards(): pl.pallas_call(functools.partial(proximal, dims), out_shape=(block, block...  2.07 us

profile of v1, /device:TPU:1, one launch (start us, length us, event | category | flops | bytes accessed | tf_op | source)
XLA Modules:
  0.0 35.3 jit_solution(3628388535587996602)
XLA Ops:
  0.6 32.6 %shard_map.59 = (f32[616,128]{1,0:T(8,128)S(1)}, f32[616,128]{1,0:T(8,128)S(1)}, f32[22,16,128]{2,1,0:T(8,128)S(1)}, f32[1,128]{1,0:T(1,128)S(1)}) custom-call(f32[4,128,16,128]{3,2,1,0:T(8,128)} %partials.1, s32[32,128]{1,0:T(8,128)} %code_bits.1, s32[32]{0:T(128)} %group_map.1, f32[16,16,128]{2,1,0:T(8,128)} %velocity.1), custom_call_target="tpu_custom_call" | custom-call | tf_op jit(solution)/shard_map/pallas_call | solution.py:577
  33.2 2.1 %shard_map.60 = (f32[16,16,128]{2,1,0:T(8,128)}, f32[16,16,128]{2,1,0:T(8,128)}) custom-call(f32[616,128]{1,0:T(8,128)S(1)} %get-tuple-element.6.va, f32[616,128]{1,0:T(8,128)S(1)} %get-tuple-element.7.ga, f32[22,16,128]{2,1,0:T(8,128)S(1)} %get-tuple-element.8.gw, f32[1,128]{1,0:T(1,128)S(1)} %get-tuple-element.9.scale_in), custom_call_target="tpu_custom_call" | custom-call | tf_op jit(solution)/shard_map/pallas_call | solution.py:623

commit v2 on v1

--- a/solution.py
+++ b/solution.py
@@ -81,12 +81,8 @@
     arb,
     in_sem,
     part_sem,
-    s1_sems,
-    r1_sems,
-    s2_sems,
-    r2_sems,
-    s3_sems,
-    r3_sems,
+    rs_send,
+    rs_recv,
     xs_sem,
     xr_sem,
     hs_sem,
@@ -95,6 +91,7 @@
     ar_sem,
     bs_sem,
     br_sem,
+    round_sem,
 ):
     nx, ny, nz, slots, bx, by, bz = dims
     win, tiles, yp, flat = geometry(dims)
@@ -158,25 +155,23 @@
         "z+": at(z=iz + 1),
     }
     both = lambda a, b: jnp.logical_and(has[a], has[b])
-    for p in plane:
-        notify(barrier, plane_device(*p))
-    for p in stack:
-        notify(barrier, stack_device(*p))
-    total = jnp.int32(len(plane) + len(stack))
-    extra = [
-        (both("y+", "z+"), at(y=iy + 1, z=iz + 1)),
-        (both("y+", "z-"), at(y=iy + 1, z=iz - 1)),
-        (both("y-", "z+"), at(y=iy - 1, z=iz + 1)),
-        (both("y-", "z-"), at(y=iy - 1, z=iz - 1)),
-        (jnp.logical_and(zl == 1, ix < nx - 1), at(x=ix + 1)),
-        (jnp.logical_and(zl == 0, ix > 0), at(x=ix - 1)),
-    ]
-    for present, device in extra:
-        total = total + present.astype(jnp.int32)
-
-        @pl.when(present)
-        def _(device=device):
-            notify(barrier, device)
+    ring_x = (at(x=block[2]), at(x=block[6]))
+    ring_y = (at(z=lax.rem(iz + 1, nz)), at(z=lax.rem(iz + nz - 1, nz)))
+    beyond = lax.rem(iy + ny + 4 * zl - 2, ny)
+    around = ring_x + ring_y + (
+        at(x=block[1]),
+        at(x=block[1], y=beyond),
+        at(y=iy + 1 - 2 * lax.rem(iy, 2)),
+    )
+
+    def greet(sem):
+        for device in around:
+            notify(sem, device)
+
+    def hear(sem):
+        pl.semaphore_wait(sem, len(around))
+
+    greet(barrier)
 
     for buffer in (za, va, ga):
         buffer[...] = jnp.zeros_like(buffer)
@@ -226,50 +221,94 @@
         lax.fori_loop(0, bx, one, 0, unroll=4)
 
     cuts = [per * k // 3 for k in range(4)]
-
-    def span(mask, k):
-        return pl.ds(block[mask] * per + cuts[k], cuts[k + 1] - cuts[k])
-
-    def hop(k, step, m, src):
-        width = cuts[k + 1] - cuts[k]
-        to = r1.at[k, m] if step == 0 else r2.at[k, m] if step == 1 else r3.at[k]
-        sends = s1_sems.at[k, m] if step == 0 else s2_sems.at[k, m] if step == 1 else s3_sems.at[k]
-        recvs = r1_sems.at[k, m] if step == 0 else r2_sems.at[k, m] if step == 1 else r3_sems.at[k]
+    sizes = [cuts[k + 1] - cuts[k] for k in range(3)]
+    lots = [(0, 0), (0, 1), (1, None), (2, None), (3, None)]
+
+    def piece(k, lot):
+        middle = (sizes[k] + 1) // 2
+        return {0: (0, middle), 1: (middle, sizes[k]), None: (0, sizes[k])}[lot[1]]
+
+    def mine(mask, k, lot):
+        low, high = piece(k, lot)
+        return pl.ds(block[mask] * per + cuts[k] + low, high - low)
+
+    def kept(k, m):
+        a, b, c = PARTS[k]
+        return (b ^ c, b, c, 0)[m]
+
+    def hop(k, step, src, dst, n):
         return pltpu.make_async_remote_copy(
             src_ref=src,
-            dst_ref=to.at[pl.ds(0, width)],
-            send_sem=sends,
-            recv_sem=recvs,
+            dst_ref=dst,
+            send_sem=rs_send.at[k, n],
+            recv_sem=rs_recv.at[k, n],
             device_id=at(x=block[PARTS[k][step]]),
             device_id_type=MESH,
         )
 
-    def kept(k):
-        a, b, c = PARTS[k]
-        return [b ^ c, b, c, 0]
-
-    def first_hop(k, m):
-        return hop(k, 0, m, psum.at[span(PARTS[k][0] ^ kept(k)[m], k)])
-
-    def second_hop(k, m):
-        return hop(k, 1, m, s2.at[k, m, pl.ds(0, cuts[k + 1] - cuts[k])])
-
-    def third_hop(k):
-        return hop(k, 2, 0, s3.at[k, pl.ds(0, cuts[k + 1] - cuts[k])])
-
-    done = set()
-    for m in range(4):
+    def first_hop(k, lot):
+        low, high = piece(k, lot)
+        src = psum.at[mine(PARTS[k][0] ^ kept(k, lot[0]), k, lot)]
+        return hop(k, 0, src, r1.at[k, lot[0], low:high], lots.index(lot))
+
+    def second_hop(k, lot):
+        low, high = piece(k, lot)
+        return hop(k, 1, s2.at[k, lot[0], low:high], r2.at[k, lot[0], low:high], 5 + lots.index(lot))
+
+    def third_hop(k, half):
+        low, high = piece(k, (0, half))
+        return hop(k, 2, s3.at[k, low:high], r3.at[k, low:high], 8 + half)
+
+    reduced = set()
+
+    def send_first(lot):
         for k in range(3):
-            mask = PARTS[k][0] ^ kept(k)[m]
-            if mask not in done:
-                done.add(mask)
+            mask = PARTS[k][0] ^ kept(k, lot[0])
+            if mask not in reduced:
+                reduced.add(mask)
                 reduce_block(mask)
-                if len(done) == 1:
-                    pl.semaphore_wait(barrier, total)
-            first_hop(k, m).start()
-    reduce_block(0)
+            first_hop(k, lot).start()
+
+    def forward(lot):
+        for k in range(3):
+            first_hop(k, lot).wait_recv()
+            low, high = piece(k, lot)
+            m = lot[0]
+            s2[k, m, low:high] = psum[mine(kept(k, m), k, lot)] + r1[k, m, low:high]
+            second_hop(k, lot).start()
+
+    reduced.add(5)
+    reduce_block(5)
+    hear(barrier)
+    for lot in lots[:4]:
+        send_first(lot)
+    greet(round_sem.at[0])
+    for mask in LOAD_ORDER:
+        if mask not in reduced:
+            reduced.add(mask)
+            reduce_block(mask)
+    hear(round_sem.at[0])
+    greet(round_sem.at[1])
+    forward(lots[0])
+    forward(lots[1])
+    send_first(lots[4])
+    hear(round_sem.at[1])
+    greet(round_sem.at[2])
+    forward(lots[2])
+    hear(round_sem.at[2])
+    greet(round_sem.at[3])
+    for half in range(2):
+        for k in range(3):
+            if half == 0:
+                first_hop(k, lots[3]).wait_recv()
+            second_hop(k, lots[half]).wait_recv()
+            low, high = piece(k, (0, half))
+            here = pl.ds(block[kept(k, 2)] * per + cuts[k] + low, high - low)
+            s3[k, low:high] = psum[here] + r1[k, 2, low:high] + r2[k, 0, low:high]
+            third_hop(k, half).start()
     v_copy.wait()
     x_send(vw, 0)
+    hear(round_sem.at[3])
 
     lane = lax.broadcasted_iota(jnp.int32, (1, bz), 1)
     group = lane // SEG
@@ -359,30 +398,12 @@
                 ),
             )
 
-    for m in range(2):
-        for k in range(3):
-            first_hop(k, m).wait_recv()
-            width = cuts[k + 1] - cuts[k]
-            s2[k, m, 0:width] = psum[span(kept(k)[m], k)] + r1[k, m, 0:width]
-            second_hop(k, m).start()
-
-    x_arrive(vw, 0)
-    prepare(0, vw)
-    send_all(0)
-
-    for k in range(3):
-        first_hop(k, 2).wait_recv()
-        second_hop(k, 0).wait_recv()
-        width = cuts[k + 1] - cuts[k]
-        mine = psum[span(kept(k)[2], k)] + r1[k, 2, 0:width]
-        s3[k, 0:width] = mine + r2[k, 0, 0:width]
-        third_hop(k).start()
-
     squares = jnp.zeros((8, bz), jnp.float32)
     for k in range(3):
-        first_hop(k, 3).wait_recv()
-        second_hop(k, 1).wait_recv()
-        third_hop(k).wait_recv()
+        first_hop(k, lots[4]).wait_recv()
+        second_hop(k, lots[2]).wait_recv()
+        for half in range(2):
+            third_hop(k, half).wait_recv()
         for j in range(cuts[k], cuts[k + 1]):
             n = j - cuts[k]
             value = psum[ix * per + j] + r1[k, 3, n] + (r2[k, 1, n] + r3[k, n])
@@ -409,14 +430,9 @@
     ara[me_a] = jnp.sum(squares, axis=0, keepdims=True)
     spread(ara, me_a, plane, plane_device, as_sem, ar_sem)
     x_send(gw, 1)
-    receive_all(0)
-    assemble(0, vw, va)
-    for k in range(3):
-        for m in range(4):
-            first_hop(k, m).wait_send()
-        for m in range(2):
-            second_hop(k, m).wait_send()
-        third_hop(k).wait_send()
+    x_arrive(vw, 0)
+    prepare(0, vw)
+    send_all(0)
     x_arrive(gw, 1)
     prepare(1, gw)
     send_all(1)
@@ -426,6 +442,15 @@
     arb[me_b] = jnp.sum(ara[...], axis=0)
     spread(arb, me_b, stack, stack_device, bs_sem, br_sem)
 
+    for k in range(3):
+        for lot in lots:
+            first_hop(k, lot).wait_send()
+        for lot in lots[:3]:
+            second_hop(k, lot).wait_send()
+        for half in range(2):
+            third_hop(k, half).wait_send()
+    receive_all(0)
+    assemble(0, vw, va)
     receive_all(1)
     assemble(1, gw, ga)
     drain(ara, plane, as_sem)
@@ -601,12 +626,8 @@
             f32((2 * ny, 1, bz)),
             dma((3,)),
             dma((nx,)),
-            dma((3, 4)),
-            dma((3, 4)),
-            dma((3, 2)),
-            dma((3, 2)),
-            dma((3,)),
-            dma((3,)),
+            dma((3, 10)),
+            dma((3, 10)),
             dma((2, 2)),
             dma((2, 2)),
             dma((2, 8)),
@@ -615,6 +636,7 @@
             dma,
             dma,
             dma,
+            pltpu.SemaphoreType.REGULAR((4,)),
         ],
         compiler_params=pltpu.CompilerParams(
             collective_id=0, has_side_effects=True

time: 35.3 us -> 32.8 us (0.929)
  Pallas kernels: 34.6 us -> 32 us
    pallas_call x1, Pallas kernels: 32.6 us -> 30 us  [shards(): pl.pallas_call(functools.partial(kernel, dims), out_shape=handed, in_spec...]
where the time goes in v2:
time: 32.8 us; the launch traced here: 32.7 us
  Pallas kernels  32 us (98%)
  between operations  0.64 us (2%)
    pallas_call x1, Pallas kernels, shards(): pl.pallas_call(functools.partial(kernel, dims), out_shape=handed, in_spec...  30 us
    pallas_call x1, Pallas kernels, shards(): pl.pallas_call(functools.partial(proximal, dims), out_shape=(block, block...  2.07 us

profile of v2, /device:TPU:1, one launch (start us, length us, event | category | flops | bytes accessed | tf_op | source)
XLA Modules:
  0.0 32.7 jit_solution(13813522536689228736)
XLA Ops:
  0.6 30.0 %shard_map.59 = (f32[616,128]{1,0:T(8,128)S(1)}, f32[616,128]{1,0:T(8,128)S(1)}, f32[22,16,128]{2,1,0:T(8,128)S(1)}, f32[1,128]{1,0:T(1,128)S(1)}) custom-call(f32[4,128,16,128]{3,2,1,0:T(8,128)} %partials.1, s32[32,128]{1,0:T(8,128)} %code_bits.1, s32[32]{0:T(128)} %group_map.1, f32[16,16,128]{2,1,0:T(8,128)} %velocity.1), custom_call_target="tpu_custom_call" | custom-call | tf_op jit(solution)/shard_map/pallas_call | solution.py:602
  30.6 2.1 %shard_map.60 = (f32[16,16,128]{2,1,0:T(8,128)}, f32[16,16,128]{2,1,0:T(8,128)}) custom-call(f32[616,128]{1,0:T(8,128)S(1)} %get-tuple-element.6.va, f32[616,128]{1,0:T(8,128)S(1)} %get-tuple-element.7.ga, f32[22,16,128]{2,1,0:T(8,128)S(1)} %get-tuple-element.8.gw, f32[1,128]{1,0:T(1,128)S(1)} %get-tuple-element.9.scale_in), custom_call_target="tpu_custom_call" | custom-call | tf_op jit(solution)/shard_map/pallas_call | solution.py:645
